TPU v7x, 32 devices: a whole 2x2x4 slice. The times are simulated.
32 devices in a mesh: shard: 8 (over z, core), rep: 4 (over y, x).
Axes of the slice: x: 2, y: 2, z: 4, core: 2. Of those that a mesh axis runs over, the one named last changes fastest.
Arguments:
- tokens: bfloat16 [12288, 5120], P(('shard', 'rep')), may hold values from -700 to 700
- norm_gain: float32 [5120], replicated, may hold values from 0.1 to 1.9
- key_bias: float32 [1024], replicated, may hold values from -4 to 4
- key_weight: bfloat16 [8192, 1024], P('shard'), may hold values from -0.078125 to 0.078125
- cotangent: bfloat16 [12288, 1024], P(('shard', 'rep')), may hold values from -40 to 40
- block_slot: int32 [40], replicated, may hold values from 0 to 63, as said below
Outputs:
- projected: bfloat16 [12288, 1024], P(('shard', 'rep'))
- token_grad: bfloat16 [12288, 5120], P(('shard', 'rep'))
- weight_grad: float32 [8192, 1024], P('shard')
- gain_grad: float32 [5120], replicated
- bias_grad: float32 [1024], replicated
Inputs may be any that keep to these rules, and one draw needn't show every extreme that they name: Entries are distinct; block b lies on the device of shard with index block_slot[b] // 8, at its local slot block_slot[b] % 8; in every draw some device holds 8 blocks.
All inputs are finite; a program needn't handle non-finite values.
Results may differ from a plain program's by a relative error of at most 0.013.
Values may be sent and summed in bfloat16 or wider, within the bound.
A program may use at most 128 MiB of HBM per device.

v0:
```python
import jax
import jax.numpy as jnp
from jax import lax
from jax.sharding import PartitionSpec as P

BLK = 128
EPS = 1e-06


def normalize(tokens, norm_gain):
    values = tokens.astype(jnp.float32)
    inv_rms = lax.rsqrt(jnp.mean(values * values, axis=-1, keepdims=True) + EPS)
    normed = (values * inv_rms * norm_gain).astype(jnp.bfloat16)
    return (values, inv_rms, normed)


def token_backward(values, inv_rms, grad_normed, norm_gain):
    scaled = grad_normed * norm_gain
    inner = jnp.mean(scaled * values, axis=-1, keepdims=True)
    return (inv_rms * (scaled - values * inv_rms * inv_rms * inner)).astype(jnp.bfloat16)


def local(tokens, norm_gain, key_bias, key_weight, cotangent, block_slot):
    values, inv_rms, normed = normalize(tokens, norm_gain)
    row_count = tokens.shape[0]
    width = tokens.shape[1]
    local_rows = key_weight.shape[0]
    shard_count = lax.axis_size("shard")
    replicas = lax.axis_size("rep")
    slot_total = shard_count * local_rows // BLK
    block_count = width // BLK
    block_of_slot = (
        jnp.full((slot_total,), -1, jnp.int32)
        .at[block_slot]
        .set(jnp.arange(block_count, dtype=jnp.int32))
    )
    present = block_of_slot >= 0
    normed_blocks = normed.reshape(row_count, block_count, BLK)
    normed_slots = jnp.take(normed_blocks, jnp.maximum(block_of_slot, 0), axis=1)
    normed_slots = jnp.where(present[None, :, None], normed_slots, jnp.zeros((), jnp.bfloat16))
    normed_slots = normed_slots.reshape(row_count, slot_total * BLK)
    piece = lax.all_gather(key_weight, "shard", axis=0, tiled=True)
    columns = normed_slots
    forward_sum = jnp.dot(columns, piece, preferred_element_type=jnp.float32)
    backward_part = lax.dot_general(
        cotangent, piece, (((1,), (1,)), ((), ())), preferred_element_type=jnp.float32
    )
    projected = (forward_sum + key_bias).astype(jnp.bfloat16)
    grad_normed = jnp.take(backward_part.reshape(row_count, slot_total, BLK), block_slot, axis=1)
    grad_normed = grad_normed.reshape(row_count, width)
    token_grad = token_backward(values, inv_rms, grad_normed, norm_gain)
    grad_scale = float(row_count * shard_count * replicas) ** (-0.5)
    columns = normed_slots
    group_sum = lax.psum_scatter(
        (
            lax.dot_general(
                columns, cotangent, (((0,), (0,)), ((), ())), preferred_element_type=jnp.float32
            )
            * grad_scale
        ).astype(jnp.bfloat16),
        "shard",
        scatter_dimension=0,
        tiled=True,
    ).astype(jnp.float32)
    gain_part = jnp.sum(grad_normed * values * inv_rms, axis=0) * grad_scale
    bias_part = jnp.sum(cotangent.astype(jnp.float32), axis=0) * grad_scale
    weight_grad = lax.psum(group_sum, "rep")
    gain_grad, bias_grad = lax.psum((gain_part, bias_part), ("shard", "rep"))
    return (projected, token_grad, weight_grad, gain_grad, bias_grad)


def solution(mesh):
    return jax.shard_map(
        local,
        mesh=mesh,
        in_specs=(
            P(("shard", "rep"), None),
            P(),
            P(),
            P("shard", None),
            P(("shard", "rep"), None),
            P(),
        ),
        out_specs=(
            P(("shard", "rep"), None),
            P(("shard", "rep"), None),
            P("shard", None),
            P(),
            P(),
        ),
        check_vma=False,
    )
```

profile of v0, /device:TPU:16, one launch (start us, length us, event | category | flops | bytes accessed | tf_op | source)
XLA Modules:
  0.0 578.5 jit_solution(7815864115164983269)
XLA Ops:
  7.2 0.0 copy-start.6
  7.2 0.0 copy-start.3
  7.2 0.0 all-gather.2.cloned.1.call-start
  7.2 0.7 all-gather.2.cloned.1.call-update
  7.9 0.0 reduce-scatter.2.cloned.1.call-start
  8.0 6.3 %copy.12 = bf16[384,5120]{0,1:T(8,128)(2,1)} copy(bf16[384,5120]{1,0:T(8,128)(2,1)} %param.6) | data formatting | bytes 7864320 | tf_op args[0]
  14.2 0.0 copy-done.6
  14.2 0.7 scatter_custom_fusion
  15.0 3.0 fusion.7
  18.1 0.1 broadcast_bitcast_fusion.2
  18.1 0.1 broadcast_bitcast_fusion
  18.2 141.7 %all-gather.2.cloned.1.call-done = bf16[8192,1024]{1,0:T(8,128)(2,1)} async-done(((bf16[1024,1024]{1,0:T(8,128)(2,1)}), bf16[8192,1024]{1,0:T(8,128)(2,1)}) %all-gather.2.cloned.1.call-update) | async-done | bytes 16777232 | tf_op jit(solution)/shard_map/all_gather | solution.py:42
  160.0 12.9 %convolution_bitcast_fusion = f32[48,64,8,128]{3,2,1,0:T(8,128)} fusion(bf16[384,1024]{1,0:T(8,128)(2,1)S(1)} %copy-done.3, bf16[8192,1024]{1,0:T(8,128)(2,1)} %all-gather.2.cloned.1.call-done), kind=kOutput, calls=%fused_computation.24 | convolution fusion | flops 6442450944 | bytes 30146560 | tf_op jit(solution)/shard_map/dot_general | solution.py:45
  172.9 10.8 %copy.20 = f32[48,64,8,128]{3,2,0,1:T(8,128)} copy(f32[48,64,8,128]{3,2,1,0:T(8,128)} %convolution_bitcast_fusion) | data formatting | bytes 25165824 | tf_op jit(solution)/shard_map/reshape | solution.py:49
  183.7 8.7 %gather_fusion.1 = f32[40,384,128]{2,1,0:T(8,128)} fusion(f32[384,64,128]{2,0,1:T(8,128)} %bitcast.34, s32[1024]{0:T(1024)S(1)} %pad_clamp_fusion), kind=kCustom, calls=%fused_computation.1 | custom fusion | bytes 15728800 | tf_op jit(solution)/shard_map/jit(_take)/gather | solution.py:49
  192.4 9.1 %copy.16 = f32[384,40,128]{0,2,1:T(8,128)} copy(f32[384,40,128]{2,0,1:T(8,128)} %bitcast.35) | data formatting | bytes 15728640 | tf_op jit(solution)/shard_map/jit(_take)/gather | solution.py:49
  201.5 8.8 %fusion.10 = (f32[5120]{0:T(1024)S(1)}, f32[384]{0:T(512)S(1)}) fusion(bf16[384,5120]{0,1:T(8,128)(2,1)} %copy.12, f32[384,40,128]{0,2,1:T(8,128)} %copy.16, f32[384]{0:T(512)S(1)} %add_rsqrt_fusion, pred[5120]{0:T(1024)(128)(4,1)S(1)} %broadcast_bitcast_fusion.2, f32[5120]{0:T(1024)S(1)} %copy-done.4), kind=kLoop, calls=%fused_computation.19 | loop fusion | flops 15723136 | bytes 11845632 | tf_op jit(solution)/shard_map/reduce_sum | solution.py:65
  210.3 5.5 fusion.6
  215.8 6.3 %copy.13 = bf16[384,40,128]{2,0,1:T(8,128)(2,1)} copy(bf16[384,40,128]{0,2,1:T(8,128)(2,1)} %bitcast.37) | data formatting | bytes 7864320 | tf_op jit(solution)/shard_map/reshape | solution.py:38
  222.1 6.1 %gather_fusion = bf16[64,384,128]{2,1,0:T(8,128)(2,1)} fusion(bf16[384,40,128]{2,0,1:T(8,128)(2,1)} %copy.13, s32[1024]{0:T(1024)S(1)} %pad_clamp_fusion.1), kind=kCustom, calls=%fused_computation | custom fusion | bytes 12583168 | tf_op jit(solution)/shard_map/jit(_take)/gather | solution.py:39
  228.2 8.6 %copy.14 = bf16[384,64,128]{0,2,1:T(8,128)(2,1)} copy(bf16[384,64,128]{2,0,1:T(8,128)(2,1)} %bitcast.36) | data formatting | bytes 12582912 | tf_op jit(solution)/shard_map/jit(_take)/gather | solution.py:39
  236.8 6.9 %fusion.12 = bf16[384,8192]{0,1:T(8,128)(2,1)S(1)} fusion(bf16[384,64,128]{0,2,1:T(8,128)(2,1)} %copy.14, pred[8192]{0:T(1024)(128)(4,1)S(1)} %get-tuple-element.18, pred[8192]{0:T(1024)(128)(4,1)S(1)} %get-tuple-element.19), kind=kLoop, calls=%fused_computation.23 | loop fusion | flops 6291456 | bytes 12599296 | tf_op jit(solution)/shard_map/jit(_where)/select_n | solution.py:40
  243.7 2.6 copy-done.2
  246.3 11.7 %multiply_convert_fusion = bf16[8192,1024]{1,0:T(8,128)(2,1)} fusion(bf16[384,8192]{0,1:T(8,128)(2,1)S(1)} %fusion.12, bf16[384,1024]{1,0:T(8,128)(2,1)S(1)} %copy-done.3), kind=kOutput, calls=%fused_computation.3 | convolution fusion | flops 6459228160 | bytes 23855104 | tf_op jit(solution)/shard_map/dot_general | solution.py:56
  258.0 0.0 reduce-scatter.2.cloned.1.call-update
  258.0 0.0 copy-start.5
  258.0 0.1 convert_reduce_fusion
  258.2 6.3 %copy.17 = bf16[384,5120]{1,0:T(8,128)(2,1)} copy(bf16[384,5120]{0,1:T(8,128)(2,1)} %get-tuple-element.14) | data formatting | bytes 7864320
  264.4 42.3 %all-reduce = (f32[5120]{0:T(1024)}, f32[1024]{0:T(1024)}) all-reduce(f32[5120]{0:T(1024)S(1)} %broadcast_multiply_fusion, f32[1024]{0:T(1024)S(1)} %broadcast_multiply_fusion.1), channel_id=1, replica_groups=mesh['shard'=8,'rep'=4] {'shard','rep'}, use_global_device_ids=true, to_apply=%region_6.7 | all-reduce | flops 6144 | bytes 49152 | tf_op jit(solution)/shard_map/psum | solution.py:68
  306.7 13.0 %add_convert_fusion = bf16[384,1024]{1,0:T(8,128)(2,1)} fusion(bf16[384,8192]{0,1:T(8,128)(2,1)} %copy-done.2, bf16[8192,1024]{1,0:T(8,128)(2,1)} %all-gather.2.cloned.1.call-done, f32[1024]{0:T(1024)S(1)} %copy-done.5), kind=kOutput, calls=%fused_computation.26 | convolution fusion | flops 6443237376 | bytes 23859200 | tf_op jit(solution)/shard_map/dot_general | solution.py:44
  319.7 105.2 %reduce-scatter.2.cloned.1.call-done = bf16[1024,1024]{1,0:T(8,128)(2,1)} async-done(((bf16[8192,1024]{1,0:T(8,128)(2,1)}), bf16[1024,1024]{1,0:T(8,128)(2,1)}) %reduce-scatter.2.cloned.1.call-update) | async-done | bytes 2097168 | tf_op jit(solution)/shard_map/reduce_scatter | solution.py:54
  424.9 146.8 %all-reduce.2 = f32[1024,1024]{1,0:T(8,128)} all-reduce(bf16[1024,1024]{1,0:T(8,128)(2,1)} %reduce-scatter.2.cloned.1.call-done), channel_id=1, replica_groups=mesh['shard'=8,'rep'=4] {'rep'}, use_global_device_ids=true, to_apply=%region_4.5 | all-reduce | flops 1048576 | bytes 6291456 | tf_op jit(solution)/shard_map/psum | solution.py:67
  (20 shorter events, 0.1 us)
Async XLA Ops:
  7.2 7.1 %copy-start.6 = (s32[40]{0:T(128)S(1)}, s32[40]{0:T(128)}, u32[]{:S(2)}) copy-start(s32[40]{0:T(128)} %param.11) | copy-start | bytes 484
  7.2 152.8 %copy-start.3 = (bf16[384,1024]{1,0:T(8,128)(2,1)S(1)}, bf16[384,1024]{1,0:T(8,128)(2,1)}, u32[]{:S(2)}) copy-start(bf16[384,1024]{1,0:T(8,128)(2,1)} %param.10) | copy-start | bytes 2359300
  7.2 152.8 %all-gather.2.cloned.1.call-start = ((), (), s32[]{:S(2)}) async-start(), calls=%async_computation.1 | async-start | bytes 18874368 | tf_op jit(solution)/shard_map/all_gather | solution.py:42
  7.9 417.0 %reduce-scatter.2.cloned.1.call-start = ((), (), s32[]{:S(2)}) async-start(), calls=%async_computation.2 | async-start | bytes 18874368 | tf_op jit(solution)/shard_map/reduce_scatter | solution.py:54
  192.4 9.1 %copy-start.4 = (f32[5120]{0:T(1024)S(1)}, f32[5120]{0:T(1024)}, u32[]{:S(2)}) copy-start(f32[5120]{0:T(1024)} %param.7) | copy-start | bytes 61444
  201.5 8.8 %copy-start = (f32[384,40,128]{0,2,1:T(8,128)S(1)}, f32[384,40,128]{0,2,1:T(8,128)}, u32[]{:S(2)}) copy-start(f32[384,40,128]{0,2,1:T(8,128)} %copy.16) | copy-start | bytes 23592964
  201.5 8.8 %copy-start.1 = (bf16[384,5120]{0,1:T(8,128)(2,1)S(1)}, bf16[384,5120]{0,1:T(8,128)(2,1)}, u32[]{:S(2)}) copy-start(bf16[384,5120]{0,1:T(8,128)(2,1)} %copy.12) | copy-start | bytes 11796484
  243.7 2.6 copy-start.2
  258.0 48.7 %copy-start.5 = (f32[1024]{0:T(1024)S(1)}, f32[1024]{0:T(1024)}, u32[]{:S(2)}) copy-start(f32[1024]{0:T(1024)} %param.8) | copy-start | bytes 12292
Sparse Core Ops, SparseCore 0:
  9.6 150.3 all-gather.1
  258.1 166.7 reduce-scatter.1
where the time goes:
time: 580 us; the launch traced here: 579 us
  waiting for transfers between devices  248 us (43%)
  blocking collectives  189 us (33%)
  local copies, waits for them, and re-layouts  65.7 us (11%)
  matrix products  37.5 us (6%)
  other arithmetic  24.4 us (4%)
  between operations  14.2 us (2%)
    psum x1, blocking collectives, local(): weight_grad = lax.psum(group_sum, 'rep')  147 us
    all_gather x1, waiting for transfers between devices, local(): piece = lax.all_gather(key_weight, 'shard', axis=0, tiled=True)  142 us
    reduce_scatter x1, waiting for transfers between devices, local(): lax.psum_scatter((lax.dot_general(columns, cotangent, (((0,), (0,)), ((),...  105 us
    psum x1, blocking collectives, local(): gain_grad, bias_grad = lax.psum((gain_part, bias_part), ('shard', 'rep'))  42.3 us
    gather x2, local copies, waits for them, and re-layouts, local(): jnp.take(backward_part.reshape(row_count, slot_total, BLK), block_slot, a...  17.8 us
    unnamed x16, local copies, waits for them, and re-layouts  15.2 us
    gather x2, local copies, waits for them, and re-layouts, local(): jnp.take(normed_blocks, jnp.maximum(block_of_slot, 0), axis=1)  14.7 us
    dot_general x1, matrix products, local(): forward_sum = jnp.dot(columns, piece, preferred_element_type=jnp.float32)  13 us
  transfers between devices with their start and end apart: 2, of which 2 were waited for; matrix products, arithmetic and copies ran while one was open for 5% of the time, Pallas kernels for 0%

commit v1 on v0

--- a/solution.py
+++ b/solution.py
@@ -5,6 +5,11 @@
 
 BLK = 128
 EPS = 1e-06
+
+
+def by_each_axis(array, inner_axis, outer_axis):
+    half = lax.psum(array, inner_axis)
+    return lax.psum(half, outer_axis)
 
 
 def normalize(tokens, norm_gain):
@@ -65,7 +70,7 @@
     gain_part = jnp.sum(grad_normed * values * inv_rms, axis=0) * grad_scale
     bias_part = jnp.sum(cotangent.astype(jnp.float32), axis=0) * grad_scale
     weight_grad = lax.psum(group_sum, "rep")
-    gain_grad, bias_grad = lax.psum((gain_part, bias_part), ("shard", "rep"))
+    gain_grad, bias_grad = by_each_axis((gain_part, bias_part), "rep", "shard")
     return (projected, token_grad, weight_grad, gain_grad, bias_grad)
 
 

time: 580 us -> 607 us (1.047); the launches traced: 579 us -> 598 us
  waiting for transfers between devices: 248 us -> 289 us
  blocking collectives: 189 us -> 168 us
    reduce_scatter x1, waiting for transfers between devices: 105 us -> 146 us  [local(): lax.psum_scatter((lax.dot_general(columns, cotangent, (((0,), (0,)), ((),...]
    psum x1, blocking collectives: 42.3 us -> 19.4 us  [by_each_axis(): return lax.psum(half, outer_axis)]
where the time goes in v1:
time: 607 us; the launch traced here: 598 us
  waiting for transfers between devices  289 us (48%)
  blocking collectives  168 us (28%)
  local copies, waits for them, and re-layouts  65.7 us (11%)
  matrix products  37.7 us (6%)
  other arithmetic  24.4 us (4%)
  between operations  14.2 us (2%)
    psum x1, blocking collectives, local(): weight_grad = lax.psum(group_sum, 'rep')  148 us
    reduce_scatter x1, waiting for transfers between devices, local(): lax.psum_scatter((lax.dot_general(columns, cotangent, (((0,), (0,)), ((),...  146 us
    all_gather x1, waiting for transfers between devices, local(): piece = lax.all_gather(key_weight, 'shard', axis=0, tiled=True)  142 us
    psum x1, blocking collectives, by_each_axis(): return lax.psum(half, outer_axis)  19.4 us
    gather x2, local copies, waits for them, and re-layouts, local(): jnp.take(backward_part.reshape(row_count, slot_total, BLK), block_slot, a...  17.8 us
    unnamed x16, local copies, waits for them, and re-layouts  15.2 us
    gather x2, local copies, waits for them, and re-layouts, local(): jnp.take(normed_blocks, jnp.maximum(block_of_slot, 0), axis=1)  14.7 us
    dot_general x1, matrix products, local(): forward_sum = jnp.dot(columns, piece, preferred_element_type=jnp.float32)  13.2 us
  transfers between devices with their start and end apart: 2, of which 2 were waited for; matrix products, arithmetic and copies ran while one was open for 5% of the time, Pallas kernels for 0%

profile of v1, /device:TPU:16, one launch (start us, length us, event | category | flops | bytes accessed | tf_op | source)
XLA Modules:
  0.0 598.5 jit_solution(10817399489784882773)
XLA Ops:
  7.2 0.0 copy-start.6
  7.2 0.0 copy-start.3
  7.2 0.0 all-gather.2.cloned.1.call-start
  7.2 0.7 all-gather.2.cloned.1.call-update
  7.9 0.0 reduce-scatter.2.cloned.1.call-start
  8.0 6.3 %copy.12 = bf16[384,5120]{0,1:T(8,128)(2,1)} copy(bf16[384,5120]{1,0:T(8,128)(2,1)} %param.6) | data formatting | bytes 7864320 | tf_op args[0]
  14.2 0.0 copy-done.6
  14.2 0.7 scatter_custom_fusion
  15.0 3.0 fusion.7
  18.1 0.1 broadcast_bitcast_fusion.2
  18.1 0.1 broadcast_bitcast_fusion
  18.2 141.7 %all-gather.2.cloned.1.call-done = bf16[8192,1024]{1,0:T(8,128)(2,1)} async-done(((bf16[1024,1024]{1,0:T(8,128)(2,1)}), bf16[8192,1024]{1,0:T(8,128)(2,1)}) %all-gather.2.cloned.1.call-update) | async-done | bytes 16777232 | tf_op jit(solution)/shard_map/all_gather | solution.py:47
  160.0 12.9 %convolution_bitcast_fusion = f32[48,64,8,128]{3,2,1,0:T(8,128)} fusion(bf16[384,1024]{1,0:T(8,128)(2,1)S(1)} %copy-done.3, bf16[8192,1024]{1,0:T(8,128)(2,1)} %all-gather.2.cloned.1.call-done), kind=kOutput, calls=%fused_computation.24 | convolution fusion | flops 6442450944 | bytes 30146560 | tf_op jit(solution)/shard_map/dot_general | solution.py:50
  172.9 10.8 %copy.20 = f32[48,64,8,128]{3,2,0,1:T(8,128)} copy(f32[48,64,8,128]{3,2,1,0:T(8,128)} %convolution_bitcast_fusion) | data formatting | bytes 25165824 | tf_op jit(solution)/shard_map/reshape | solution.py:54
  183.7 8.7 %gather_fusion.1 = f32[40,384,128]{2,1,0:T(8,128)} fusion(f32[384,64,128]{2,0,1:T(8,128)} %bitcast.34, s32[1024]{0:T(1024)S(1)} %pad_clamp_fusion), kind=kCustom, calls=%fused_computation.1 | custom fusion | bytes 15728800 | tf_op jit(solution)/shard_map/jit(_take)/gather | solution.py:54
  192.4 9.1 %copy.16 = f32[384,40,128]{0,2,1:T(8,128)} copy(f32[384,40,128]{2,0,1:T(8,128)} %bitcast.35) | data formatting | bytes 15728640 | tf_op jit(solution)/shard_map/jit(_take)/gather | solution.py:54
  201.5 8.8 %fusion.10 = (f32[5120]{0:T(1024)S(1)}, f32[384]{0:T(512)S(1)}) fusion(bf16[384,5120]{0,1:T(8,128)(2,1)} %copy.12, f32[384,40,128]{0,2,1:T(8,128)} %copy.16, f32[384]{0:T(512)S(1)} %add_rsqrt_fusion, pred[5120]{0:T(1024)(128)(4,1)S(1)} %broadcast_bitcast_fusion.2, f32[5120]{0:T(1024)S(1)} %copy-done.4), kind=kLoop, calls=%fused_computation.19 | loop fusion | flops 15723136 | bytes 11845632 | tf_op jit(solution)/shard_map/reduce_sum | solution.py:70
  210.3 5.5 fusion.6
  215.8 6.3 %copy.13 = bf16[384,40,128]{2,0,1:T(8,128)(2,1)} copy(bf16[384,40,128]{0,2,1:T(8,128)(2,1)} %bitcast.37) | data formatting | bytes 7864320 | tf_op jit(solution)/shard_map/reshape | solution.py:43
  222.1 6.1 %gather_fusion = bf16[64,384,128]{2,1,0:T(8,128)(2,1)} fusion(bf16[384,40,128]{2,0,1:T(8,128)(2,1)} %copy.13, s32[1024]{0:T(1024)S(1)} %pad_clamp_fusion.1), kind=kCustom, calls=%fused_computation | custom fusion | bytes 12583168 | tf_op jit(solution)/shard_map/jit(_take)/gather | solution.py:44
  228.2 8.6 %copy.14 = bf16[384,64,128]{0,2,1:T(8,128)(2,1)} copy(bf16[384,64,128]{2,0,1:T(8,128)(2,1)} %bitcast.36) | data formatting | bytes 12582912 | tf_op jit(solution)/shard_map/jit(_take)/gather | solution.py:44
  236.8 6.9 %fusion.12 = bf16[384,8192]{0,1:T(8,128)(2,1)S(1)} fusion(bf16[384,64,128]{0,2,1:T(8,128)(2,1)} %copy.14, pred[8192]{0:T(1024)(128)(4,1)S(1)} %get-tuple-element.21, pred[8192]{0:T(1024)(128)(4,1)S(1)} %get-tuple-element.22), kind=kLoop, calls=%fused_computation.23 | loop fusion | flops 6291456 | bytes 12599296 | tf_op jit(solution)/shard_map/jit(_where)/select_n | solution.py:45
  243.7 2.6 copy-done.2
  246.3 11.7 %multiply_convert_fusion = bf16[8192,1024]{1,0:T(8,128)(2,1)} fusion(bf16[384,8192]{0,1:T(8,128)(2,1)S(1)} %fusion.12, bf16[384,1024]{1,0:T(8,128)(2,1)S(1)} %copy-done.3), kind=kOutput, calls=%fused_computation.3 | convolution fusion | flops 6459228160 | bytes 23855104 | tf_op jit(solution)/shard_map/dot_general | solution.py:61
  258.0 0.0 reduce-scatter.2.cloned.1.call-update
  258.0 0.0 copy-start.5
  258.0 0.1 convert_reduce_fusion
  258.2 6.3 %copy.17 = bf16[384,5120]{1,0:T(8,128)(2,1)} copy(bf16[384,5120]{0,1:T(8,128)(2,1)} %get-tuple-element.17) | data formatting | bytes 7864320
  264.4 13.2 %add_convert_fusion = bf16[384,1024]{1,0:T(8,128)(2,1)} fusion(bf16[384,8192]{0,1:T(8,128)(2,1)} %copy-done.2, bf16[8192,1024]{1,0:T(8,128)(2,1)} %all-gather.2.cloned.1.call-done, f32[1024]{0:T(1024)S(1)} %copy-done.5), kind=kOutput, calls=%fused_computation.26 | convolution fusion | flops 6443237376 | bytes 23859200 | tf_op jit(solution)/shard_map/dot_general | solution.py:49
  277.6 146.2 %reduce-scatter.2.cloned.1.call-done = bf16[1024,1024]{1,0:T(8,128)(2,1)} async-done(((bf16[8192,1024]{1,0:T(8,128)(2,1)}), bf16[1024,1024]{1,0:T(8,128)(2,1)}) %reduce-scatter.2.cloned.1.call-update) | async-done | bytes 2097168 | tf_op jit(solution)/shard_map/reduce_scatter | solution.py:59
  423.9 148.4 %all-reduce.3 = (f32[1024,1024]{1,0:T(8,128)}, f32[5120]{0:T(1024)S(1)}, f32[1024]{0:T(1024)S(1)}) all-reduce(bf16[1024,1024]{1,0:T(8,128)(2,1)} %reduce-scatter.2.cloned.1.call-done, f32[5120]{0:T(1024)S(1)} %broadcast_multiply_fusion, f32[1024]{0:T(1024)S(1)} %broadcast_multiply_fusion.1), channel_id=1, replica_groups=mesh['shard'=8,'rep'=4] {'rep'}, use_global_device_ids=true, to_apply=%region_4.5 | all-reduce | flops 1054720 | bytes 6340608 | tf_op jit(solution)/shard_map/psum | solution.py:72
  572.3 19.4 %all-reduce = (f32[5120]{0:T(1024)}, f32[1024]{0:T(1024)}) all-reduce(f32[5120]{0:T(1024)S(1)} %get-tuple-element.15, f32[1024]{0:T(1024)S(1)} %get-tuple-element.16), channel_id=1, replica_groups=mesh['shard'=8,'rep'=4] {'shard'}, use_global_device_ids=true, to_apply=%region_7.8 | all-reduce | flops 6144 | bytes 49152 | tf_op jit(solution)/shard_map/psum | solution.py:12
  (20 shorter events, 0.1 us)
Async XLA Ops:
  7.2 7.1 %copy-start.6 = (s32[40]{0:T(128)S(1)}, s32[40]{0:T(128)}, u32[]{:S(2)}) copy-start(s32[40]{0:T(128)} %param.11) | copy-start | bytes 484
  7.2 152.8 %copy-start.3 = (bf16[384,1024]{1,0:T(8,128)(2,1)S(1)}, bf16[384,1024]{1,0:T(8,128)(2,1)}, u32[]{:S(2)}) copy-start(bf16[384,1024]{1,0:T(8,128)(2,1)} %param.10) | copy-start | bytes 2359300
  7.2 152.8 %all-gather.2.cloned.1.call-start = ((), (), s32[]{:S(2)}) async-start(), calls=%async_computation.1 | async-start | bytes 18874368 | tf_op jit(solution)/shard_map/all_gather | solution.py:47
  7.9 415.9 %reduce-scatter.2.cloned.1.call-start = ((), (), s32[]{:S(2)}) async-start(), calls=%async_computation.2 | async-start | bytes 18874368 | tf_op jit(solution)/shard_map/reduce_scatter | solution.py:59
  192.4 9.1 %copy-start.4 = (f32[5120]{0:T(1024)S(1)}, f32[5120]{0:T(1024)}, u32[]{:S(2)}) copy-start(f32[5120]{0:T(1024)} %param.7) | copy-start | bytes 61444
  201.5 8.8 %copy-start = (f32[384,40,128]{0,2,1:T(8,128)S(1)}, f32[384,40,128]{0,2,1:T(8,128)}, u32[]{:S(2)}) copy-start(f32[384,40,128]{0,2,1:T(8,128)} %copy.16) | copy-start | bytes 23592964
  201.5 8.8 %copy-start.1 = (bf16[384,5120]{0,1:T(8,128)(2,1)S(1)}, bf16[384,5120]{0,1:T(8,128)(2,1)}, u32[]{:S(2)}) copy-start(bf16[384,5120]{0,1:T(8,128)(2,1)} %copy.12) | copy-start | bytes 11796484
  243.7 2.6 copy-start.2
  258.0 6.4 %copy-start.5 = (f32[1024]{0:T(1024)S(1)}, f32[1024]{0:T(1024)}, u32[]{:S(2)}) copy-start(f32[1024]{0:T(1024)} %param.8) | copy-start | bytes 12292
Sparse Core Ops, SparseCore 0:
  9.6 150.3 all-gather.1
  258.1 165.6 reduce-scatter.1
